TPU v7x, 32 devices: a whole 2x2x4 slice. The times are simulated.
32 devices in a mesh: row: 8 (over y, x, core), col: 4 (over z).
Axes of the slice: x: 2, y: 2, z: 4, core: 2. Of those that a mesh axis runs over, the one named last changes fastest.
Arguments:
- right_sides: float32 [8, 8192, 128], P(None, ('row', 'col')), may hold values from -6 to 6
- factor_head: bfloat16 [8, 8192, 4, 1024], P(None, 'row', None, 'col'), may hold values from -0.1875 to 0.1875
- class_head: int32 [8, 8, 4], P(None, 'row'), may hold values from 0 to 2
- scale_head: float32 [8, 8, 4], P(None, 'row'), may hold values from 0.25 to 2
- inverse_head: float32 [4, 1024, 1024], P(None, 'col'), as said below
- factor_tail: bfloat16 [4, 1024, 8, 8192], P(None, 'col', None, 'row'), may hold values from -0.1875 to 0.1875
- class_tail: int32 [4, 8, 8], P(None, None, 'row'), may hold values from 0 to 2
- scale_tail: float32 [4, 8, 8], P(None, None, 'row'), may hold values from 0.25 to 2
- inverse_tail: float32 [4, 1024, 1024], P(None, None, 'col'), as said below
Outputs:
- solved_head: float32 [4, 1024, 128], P(None, 'col')
- solved_tail: float32 [4, 1024, 128], P(None, 'col')
- remainder: float32 [8, 8192, 128], P(None, ('row', 'col'))
Inputs may be any that keep to these rules, and one draw needn't show every extreme that they name: `class_head`: 0, 1, 2 name the float32, bfloat16 and scaled bfloat16 classes. `class_tail`: 0, 1, 2 name the float32, bfloat16 and scaled bfloat16 classes. `inverse_head`: every tile is lower triangular with a diagonal of 1 to 2. `inverse_tail`: every tile is lower triangular with a diagonal of 1 to 2.
All inputs are finite; a program needn't handle non-finite values.
Results may differ from a plain program's by a relative error of at most 0.008.
Values sent between devices are 32-bit elements; how exact they have to be, the bound alone decides.
A program may use at most 128 MiB of HBM per device.

v0:
```python
import jax
import jax.numpy as jnp
from jax import lax
from jax.sharding import PartitionSpec as P


def from_root(block, axis, owner):
    block = jnp.where(lax.axis_index(axis) == owner, block, jnp.zeros_like(block))
    return lax.psum(block, axis)


def tile_terms(stored, classes, scales, solved, form):
    short_piece = solved.astype(jnp.bfloat16)
    exact_term = jnp.einsum(
        form, stored.astype(jnp.float32), solved, precision=lax.Precision.HIGHEST
    )
    short_term = jnp.einsum(form, stored, short_piece, preferred_element_type=jnp.float32)
    classes = classes[:, None, None]
    scales = scales[:, None, None]
    return jnp.where(
        classes == 0, exact_term, jnp.where(classes == 1, short_term, scales * short_term)
    )


def solve_tile(partial_value, right_share, owner_row, invert):
    share_rows = right_share.shape[0]
    placed = lax.dynamic_update_slice_in_dim(
        jnp.zeros(partial_value.shape, jnp.float32),
        right_share,
        lax.axis_index("col") * share_rows,
        0,
    )
    summed = lax.psum(partial_value - placed, "col")
    solved = invert(-summed)
    return from_root(solved, "row", owner_row)


def on_device(
    right_sides,
    factor_head,
    class_head,
    scale_head,
    inverse_head,
    factor_tail,
    class_tail,
    scale_tail,
    inverse_tail,
):
    n_row = lax.axis_size("row")
    slots = right_sides.shape[0]
    ntiles = slots * n_row
    window = inverse_head.shape[0]
    tile_rows = factor_head.shape[1]
    tile_ids = jnp.arange(slots, dtype=jnp.int32) * n_row + lax.axis_index("row")
    updates = jnp.zeros((slots, tile_rows, right_sides.shape[2]), jnp.float32)
    heads = []
    for step in range(window):
        slot_k, row_k = divmod(step, n_row)
        inverse_rows = inverse_head[step]

        def invert_head(value, inverse_rows=inverse_rows):
            return jnp.dot(
                inverse_rows,
                value,
                precision=lax.Precision.HIGHEST,
                preferred_element_type=jnp.float32,
            )

        solved = solve_tile(updates[slot_k], right_sides[slot_k], row_k, invert_head)
        heads.append(solved)
        terms = tile_terms(
            factor_head[:, :, step, :],
            class_head[:, 0, step],
            scale_head[:, 0, step],
            solved,
            "lab,bn->lan",
        )
        active = (tile_ids > step)[:, None, None]
        updates = updates + jnp.where(active, terms, jnp.float32(0.0))
    tails = [None] * window
    for step in range(window):
        target = ntiles - 1 - step
        position = window - 1 - step
        slot_j, row_j = divmod(target, n_row)
        inverse_cols = inverse_tail[position]

        def invert_tail(value, inverse_cols=inverse_cols):
            return jnp.dot(
                inverse_cols.T,
                value,
                precision=lax.Precision.HIGHEST,
                preferred_element_type=jnp.float32,
            )

        solved = solve_tile(updates[slot_j], right_sides[slot_j], row_j, invert_tail)
        tails[position] = solved
        terms = tile_terms(
            factor_tail[position],
            class_tail[position, :, 0],
            scale_tail[position, :, 0],
            solved,
            "alb,an->lbn",
        )
        active = (tile_ids < target)[:, None, None]
        updates = updates + jnp.where(active, terms, jnp.float32(0.0))
    summed = lax.psum_scatter(updates, "col", scatter_dimension=1, tiled=True)
    return (jnp.stack(heads), jnp.stack(tails), right_sides - summed)


def solution(mesh):
    return jax.shard_map(
        on_device,
        mesh=mesh,
        in_specs=(
            P(None, ("row", "col"), None),
            P(None, "row", None, "col"),
            P(None, "row", None),
            P(None, "row", None),
            P(None, "col", None),
            P(None, "col", None, "row"),
            P(None, None, "row"),
            P(None, None, "row"),
            P(None, None, "col"),
        ),
        out_specs=(P(None, "col", None), P(None, "col", None), P(None, ("row", "col"), None)),
        check_vma=False,
    )
```

profile of v0, /device:TPU:0, one launch (start us, length us, event | category | flops | bytes accessed | tf_op | source)
XLA Modules:
  0.0 989.1 jit_solution(2727695291262709679)
XLA Ops:
  9.8 41.2 %fusion.101 = (bf16[8,1024,1,256]{3,2,1,0:T(2,128)(2,1)}, bf16[8,1024,1,256]{3,2,1,0:T(2,128)(2,1)}, bf16[8,1024,1,256]{3,2,1,0:T(2,128)(2,1)}, bf16[8,1024,1,256]{3,2,1,0:T(2,128)(2,1)}) fusion(bf16[8,1024,4,256]{3,2,1,0:T(4,128)(2,1)} %param.10), kind=kLoop, calls=%fused_computation.170 | loop fusion | bytes 33554432 | tf_op jit(solution)/shard_map/slice | solution.py:72
  55.5 55.1 %all-reduce.19.cloned.1.call-done = f32[256,128]{0,1:T(8,128)} async-done(((f32[256,128]{0,1:T(8,128)}), f32[256,128]{0,1:T(8,128)}) %all-reduce.19.cloned.1.call-update) | async-done | bytes 131088 | tf_op jit(solution)/shard_map/psum | solution.py:9
  110.6 7.9 fusion.31
  123.0 38.1 %all-reduce.21.cloned.1.call-done = f32[1024,128]{0,1:T(8,128)} async-done(((f32[1024,128]{0,1:T(8,128)}), f32[1024,128]{0,1:T(8,128)}) %all-reduce.21.cloned.1.call-update) | async-done | bytes 524304 | tf_op jit(solution)/shard_map/psum | solution.py:33
  164.6 53.3 %all-reduce.23.cloned.1.call-done = f32[256,128]{0,1:T(8,128)} async-done(((f32[256,128]{0,1:T(8,128)}), f32[256,128]{0,1:T(8,128)}) %all-reduce.23.cloned.1.call-update) | async-done | bytes 131088 | tf_op jit(solution)/shard_map/psum | solution.py:9
  217.9 7.8 fusion.32
  225.7 5.0 fusion.4
  233.6 38.2 %all-reduce.25.cloned.1.call-done = f32[1024,128]{0,1:T(8,128)} async-done(((f32[1024,128]{0,1:T(8,128)}), f32[1024,128]{0,1:T(8,128)}) %all-reduce.25.cloned.1.call-update) | async-done | bytes 524304 | tf_op jit(solution)/shard_map/psum | solution.py:33
  275.1 53.5 %all-reduce.27.cloned.1.call-done = f32[256,128]{0,1:T(8,128)} async-done(((f32[256,128]{0,1:T(8,128)}), f32[256,128]{0,1:T(8,128)}) %all-reduce.27.cloned.1.call-update) | async-done | bytes 131088 | tf_op jit(solution)/shard_map/psum | solution.py:9
  328.6 7.8 fusion.33
  336.4 5.0 fusion.7
  344.5 38.0 %all-reduce.29.cloned.1.call-done = f32[1024,128]{0,1:T(8,128)} async-done(((f32[1024,128]{0,1:T(8,128)}), f32[1024,128]{0,1:T(8,128)}) %all-reduce.29.cloned.1.call-update) | async-done | bytes 524304 | tf_op jit(solution)/shard_map/psum | solution.py:33
  386.1 53.2 %all-reduce.31.cloned.1.call-done = f32[256,128]{0,1:T(8,128)} async-done(((f32[256,128]{0,1:T(8,128)}), f32[256,128]{0,1:T(8,128)}) %all-reduce.31.cloned.1.call-update) | async-done | bytes 131088 | tf_op jit(solution)/shard_map/psum | solution.py:9
  439.4 7.8 fusion.34
  455.0 12.3 %fusion.100 = (bf16[1,256,8,1024]{3,2,1,0:T(8,128)(2,1)}, bf16[1,256,8,1024]{3,2,1,0:T(8,128)(2,1)}, bf16[1,256,8,1024]{3,2,1,0:T(8,128)(2,1)}, bf16[1,256,8,1024]{3,2,1,0:T(8,128)(2,1)}) fusion(bf16[4,256,8,1024]{3,2,1,0:T(8,128)(2,1)} %param.14), kind=kLoop, calls=%fused_computation.169 | loop fusion | bytes 33554432 | tf_op jit(solution)/shard_map/slice | solution.py:98
  467.3 25.8 %all-reduce.33.cloned.1.call-done = f32[1024,128]{0,1:T(8,128)} async-done(((f32[1024,128]{0,1:T(8,128)}), f32[1024,128]{0,1:T(8,128)}) %all-reduce.33.cloned.1.call-update) | async-done | bytes 524304 | tf_op jit(solution)/shard_map/psum | solution.py:33
  495.9 54.0 %all-reduce.35.cloned.1.call-done = f32[256,128]{0,1:T(8,128)} async-done(((f32[256,128]{0,1:T(8,128)}), f32[256,128]{0,1:T(8,128)}) %all-reduce.35.cloned.1.call-update) | async-done | bytes 131088 | tf_op jit(solution)/shard_map/psum | solution.py:9
  549.9 7.3 fusion.23
  557.2 7.2 fusion.13
  567.4 38.0 %all-reduce.37.cloned.1.call-done = f32[1024,128]{0,1:T(8,128)} async-done(((f32[1024,128]{0,1:T(8,128)}), f32[1024,128]{0,1:T(8,128)}) %all-reduce.37.cloned.1.call-update) | async-done | bytes 524304 | tf_op jit(solution)/shard_map/psum | solution.py:33
  608.2 54.0 %all-reduce.39.cloned.1.call-done = f32[256,128]{0,1:T(8,128)} async-done(((f32[256,128]{0,1:T(8,128)}), f32[256,128]{0,1:T(8,128)}) %all-reduce.39.cloned.1.call-update) | async-done | bytes 131088 | tf_op jit(solution)/shard_map/psum | solution.py:9
  662.2 7.3 fusion.25
  669.6 7.2 fusion.16
  679.9 37.9 %all-reduce.41.cloned.1.call-done = f32[1024,128]{0,1:T(8,128)} async-done(((f32[1024,128]{0,1:T(8,128)}), f32[1024,128]{0,1:T(8,128)}) %all-reduce.41.cloned.1.call-update) | async-done | bytes 524304 | tf_op jit(solution)/shard_map/psum | solution.py:33
  720.5 54.0 %all-reduce.43.cloned.1.call-done = f32[256,128]{0,1:T(8,128)} async-done(((f32[256,128]{0,1:T(8,128)}), f32[256,128]{0,1:T(8,128)}) %all-reduce.43.cloned.1.call-update) | async-done | bytes 131088 | tf_op jit(solution)/shard_map/psum | solution.py:9
  774.5 7.3 fusion.27
  781.9 7.2 fusion.19
  792.3 37.9 %all-reduce.45.cloned.1.call-done = f32[1024,128]{0,1:T(8,128)} async-done(((f32[1024,128]{0,1:T(8,128)}), f32[1024,128]{0,1:T(8,128)}) %all-reduce.45.cloned.1.call-update) | async-done | bytes 524304 | tf_op jit(solution)/shard_map/psum | solution.py:33
  833.0 54.0 %all-reduce.47.cloned.1.call-done = f32[256,128]{0,1:T(8,128)} async-done(((f32[256,128]{0,1:T(8,128)}), f32[256,128]{0,1:T(8,128)}) %all-reduce.47.cloned.1.call-update) | async-done | bytes 131088 | tf_op jit(solution)/shard_map/psum | solution.py:9
  887.0 7.3 fusion.29
  894.3 8.8 fusion.22
  905.2 74.3 %reduce-scatter.2.cloned.1.call-done = f32[8,256,128]{1,2,0:T(8,128)} async-done(((f32[8,1024,128]{1,2,0:T(8,128)}), f32[8,256,128]{1,2,0:T(8,128)}) %reduce-scatter.2.cloned.1.call-update) | async-done | bytes 1048592 | tf_op jit(solution)/shard_map/reduce_scatter | solution.py:106
  (138 shorter events, 60.7 us)
Async XLA Ops:
  7.2 45.0 %all-reduce.17.cloned.1.call-start = ((), (), s32[]{:S(2)}) async-start(), calls=%async_computation.1 | async-start | bytes 1048576 | tf_op jit(solution)/shard_map/psum | solution.py:33
  9.7 41.3 %copy-start.29 = (f32[8,1,4]{0,2,1:T(4,128)S(1)}, f32[8,1,4]{0,2,1:T(4,128)}, u32[]{:S(2)}) copy-start(f32[8,1,4]{0,2,1:T(4,128)} %param.12) | copy-start | bytes 388
  9.7 41.3 %copy-start.27 = (s32[8,1,4]{0,2,1:T(4,128)S(1)}, s32[8,1,4]{0,2,1:T(4,128)}, u32[]{:S(2)}) copy-start(s32[8,1,4]{0,2,1:T(4,128)} %param.11) | copy-start | bytes 388
  9.7 100.9 %all-reduce.19.cloned.1.call-start = ((), (), s32[]{:S(2)}) async-start(), calls=%async_computation.2 | async-start | bytes 262144 | tf_op jit(solution)/shard_map/psum | solution.py:9
  55.4 105.7 %all-reduce.21.cloned.1.call-start = ((), (), s32[]{:S(2)}) async-start(), calls=%async_computation.3 | async-start | bytes 1048576 | tf_op jit(solution)/shard_map/psum | solution.py:33
  110.6 7.9 copy-start.4
  110.6 7.9 copy-start.19
  123.0 94.9 %all-reduce.23.cloned.1.call-start = ((), (), s32[]{:S(2)}) async-start(), calls=%async_computation.4 | async-start | bytes 262144 | tf_op jit(solution)/shard_map/psum | solution.py:9
  164.4 107.4 %all-reduce.25.cloned.1.call-start = ((), (), s32[]{:S(2)}) async-start(), calls=%async_computation.5 | async-start | bytes 1048576 | tf_op jit(solution)/shard_map/psum | solution.py:33
  217.9 7.8 copy-start.18
  217.9 7.8 copy-start.20
  233.6 95.0 %all-reduce.27.cloned.1.call-start = ((), (), s32[]{:S(2)}) async-start(), calls=%async_computation.6 | async-start | bytes 262144 | tf_op jit(solution)/shard_map/psum | solution.py:9
  275.0 107.4 %all-reduce.29.cloned.1.call-start = ((), (), s32[]{:S(2)}) async-start(), calls=%async_computation.7 | async-start | bytes 1048576 | tf_op jit(solution)/shard_map/psum | solution.py:33
  328.6 7.8 copy-start.12
  328.6 7.8 copy-start.21
  336.4 7.9 copy-start.30
  336.4 7.9 copy-start.28
  344.3 95.1 %all-reduce.31.cloned.1.call-start = ((), (), s32[]{:S(2)}) async-start(), calls=%async_computation.8 | async-start | bytes 262144 | tf_op jit(solution)/shard_map/psum | solution.py:9
  385.7 107.4 %all-reduce.33.cloned.1.call-start = ((), (), s32[]{:S(2)}) async-start(), calls=%async_computation.9 | async-start | bytes 1048576 | tf_op jit(solution)/shard_map/psum | solution.py:33
  439.4 7.8 copy-start.6
  439.4 7.8 copy-start.22
  455.0 94.9 %all-reduce.35.cloned.1.call-start = ((), (), s32[]{:S(2)}) async-start(), calls=%async_computation.10 | async-start | bytes 262144 | tf_op jit(solution)/shard_map/psum | solution.py:9
  495.8 109.6 %all-reduce.37.cloned.1.call-start = ((), (), s32[]{:S(2)}) async-start(), calls=%async_computation.11 | async-start | bytes 1048576 | tf_op jit(solution)/shard_map/psum | solution.py:33
  549.9 7.3 copy-start.23
  567.2 95.0 %all-reduce.39.cloned.1.call-start = ((), (), s32[]{:S(2)}) async-start(), calls=%async_computation.12 | async-start | bytes 262144 | tf_op jit(solution)/shard_map/psum | solution.py:9
  608.1 109.6 %all-reduce.41.cloned.1.call-start = ((), (), s32[]{:S(2)}) async-start(), calls=%async_computation.13 | async-start | bytes 1048576 | tf_op jit(solution)/shard_map/psum | solution.py:33
  662.2 7.3 copy-start.24
  679.6 94.9 %all-reduce.43.cloned.1.call-start = ((), (), s32[]{:S(2)}) async-start(), calls=%async_computation.14 | async-start | bytes 262144 | tf_op jit(solution)/shard_map/psum | solution.py:9
  720.5 109.7 %all-reduce.45.cloned.1.call-start = ((), (), s32[]{:S(2)}) async-start(), calls=%async_computation.15 | async-start | bytes 1048576 | tf_op jit(solution)/shard_map/psum | solution.py:33
  792.0 95.0 %all-reduce.47.cloned.1.call-start = ((), (), s32[]{:S(2)}) async-start(), calls=%async_computation.16 | async-start | bytes 262144 | tf_op jit(solution)/shard_map/psum | solution.py:9
  832.9 146.6 %reduce-scatter.2.cloned.1.call-start = ((), (), s32[]{:S(2)}) async-start(), calls=%async_computation.17 | async-start | bytes 5242880 | tf_op jit(solution)/shard_map/reduce_scatter | solution.py:106
  887.0 7.3 copy-start.26
  (16 other events, 79.9 us)
Sparse Core Ops, SparseCore 0:
  10.9 41.2 all-reduce.16
  55.8 54.7 all-reduce.18
  123.1 37.9 all-reduce.20
  164.6 53.2 all-reduce.22
  233.7 38.0 all-reduce.24
  275.3 53.2 all-reduce.26
  344.4 37.9 all-reduce.28
  386.0 53.2 all-reduce.30
  455.1 37.9 all-reduce.32
  496.6 53.2 all-reduce.34
  567.3 38.0 all-reduce.36
  608.9 53.2 all-reduce.38
  679.7 37.9 all-reduce.40
  721.2 53.2 all-reduce.42
  792.1 38.0 all-reduce.44
  833.6 53.2 all-reduce.46
  903.2 76.1 reduce-scatter.1
where the time goes:
time: 996 us; the launch traced here: 989 us
  waiting for transfers between devices  761 us (76%)
  matrix products  131 us (13%)
  local copies, waits for them, and re-layouts  72.4 us (7%)
  between operations  15 us (2%)
    psum x8, waiting for transfers between devices, from_root(): return lax.psum(block, axis)  431 us
    psum x8, waiting for transfers between devices, solve_tile(): summed = lax.psum(partial_value - placed, 'col')  255 us
    reduce_scatter x1, waiting for transfers between devices, on_device(): summed = lax.psum_scatter(updates, 'col', scatter_dimension=1, tiled=True)  74.3 us
    dot_general x8, matrix products, tile_terms(): jnp.einsum(form, stored.astype(jnp.float32), solved, precision=lax.Precis...  61.5 us
    dot_general x8, matrix products, tile_terms(): jnp.einsum(form, stored, short_piece, preferred_element_type=jnp.float32)  45.7 us
    slice x1, local copies, waits for them, and re-layouts, on_device(): factor_head[:, :, step, :]  41.2 us
  transfers between devices with their start and end apart: 17, of which 17 were waited for; matrix products, arithmetic and copies ran while one was open for 6% of the time, Pallas kernels for 0%

commit v1 on v0

--- a/solution.py
+++ b/solution.py
@@ -30,7 +30,7 @@
         lax.axis_index("col") * share_rows,
         0,
     )
-    summed = lax.psum(partial_value - placed, "col")
+    summed = jnp.sum(lax.all_gather(partial_value - placed, "col"), axis=0)
     solved = invert(-summed)
     return from_root(solved, "row", owner_row)
 

time: 996 us -> 1070 us (1.074)
  waiting for transfers between devices: 761 us -> 799 us
  local copies, waits for them, and re-layouts: 72.4 us -> 97.4 us
  other arithmetic: 8.37 us -> 19.5 us
    all_gather x0 -> x8, waiting for transfers between devices: none -> 307 us  [solve_tile(): summed = jnp.sum(lax.all_gather(partial_value - placed, 'col'), axis=0)]
    psum x8 -> x0, waiting for transfers between devices: 255 us -> none  [solve_tile(): summed = lax.psum(partial_value - placed, 'col')]
    all_gather x0 -> x8, local copies, waits for them, and re-layouts: none -> 21.4 us  [solve_tile(): summed = jnp.sum(lax.all_gather(partial_value - placed, 'col'), axis=0)]
    psum x8, waiting for transfers between devices: 431 us -> 418 us  [from_root(): return lax.psum(block, axis)]
where the time goes in v1:
time: 1070 us; the launch traced here: 1060 us
  waiting for transfers between devices  799 us (75%)
  matrix products  130 us (12%)
  local copies, waits for them, and re-layouts  97.4 us (9%)
  other arithmetic  19.5 us (2%)
  between operations  15.2 us (1%)
    psum x8, waiting for transfers between devices, from_root(): return lax.psum(block, axis)  418 us
    all_gather x8, waiting for transfers between devices, solve_tile(): summed = jnp.sum(lax.all_gather(partial_value - placed, 'col'), axis=0)  307 us
    reduce_scatter x1, waiting for transfers between devices, on_device(): summed = lax.psum_scatter(updates, 'col', scatter_dimension=1, tiled=True)  73.4 us
    dot_general x8, matrix products, tile_terms(): jnp.einsum(form, stored.astype(jnp.float32), solved, precision=lax.Precis...  61.5 us
    dot_general x8, matrix products, tile_terms(): jnp.einsum(form, stored, short_piece, preferred_element_type=jnp.float32)  45.7 us
    slice x1, local copies, waits for them, and re-layouts, on_device(): factor_head[:, :, step, :]  41.4 us
  transfers between devices with their start and end apart: 17, of which 17 were waited for; matrix products, arithmetic and copies ran while one was open for 6% of the time, Pallas kernels for 0%

profile of v1, /device:TPU:0, one launch (start us, length us, event | category | flops | bytes accessed | tf_op | source)
XLA Modules:
  0.0 1062.9 jit_solution(10592684906575062649)
XLA Ops:
  10.5 41.4 %fusion.101 = (bf16[8,1024,1,256]{3,2,1,0:T(2,128)(2,1)}, bf16[8,1024,1,256]{3,2,1,0:T(2,128)(2,1)}, bf16[8,1024,1,256]{3,2,1,0:T(2,128)(2,1)}, bf16[8,1024,1,256]{3,2,1,0:T(2,128)(2,1)}) fusion(bf16[8,1024,4,256]{3,2,1,0:T(4,128)(2,1)} %param.10), kind=kLoop, calls=%fused_computation.170 | loop fusion | bytes 33554432 | tf_op jit(solution)/shard_map/slice | solution.py:72
  51.9 6.6 all-gather.17.cloned.1.call-done
  65.7 52.4 %all-reduce.9.cloned.1.call-done = f32[256,128]{0,1:T(8,128)} async-done(((f32[256,128]{0,1:T(8,128)}), f32[256,128]{0,1:T(8,128)}) %all-reduce.9.cloned.1.call-update) | async-done | bytes 131088 | tf_op jit(solution)/shard_map/psum | solution.py:9
  118.0 7.9 fusion.31
  130.7 44.9 %all-gather.19.cloned.1.call-done = f32[4096,128]{0,1:T(8,128)} async-done(((f32[1024,128]{0,1:T(8,128)}), f32[4096,128]{0,1:T(8,128)}) %all-gather.19.cloned.1.call-update) | async-done | bytes 2097168 | tf_op jit(solution)/shard_map/all_gather | solution.py:33
  182.8 52.4 %all-reduce.11.cloned.1.call-done = f32[256,128]{0,1:T(8,128)} async-done(((f32[256,128]{0,1:T(8,128)}), f32[256,128]{0,1:T(8,128)}) %all-reduce.11.cloned.1.call-update) | async-done | bytes 131088 | tf_op jit(solution)/shard_map/psum | solution.py:9
  235.2 7.8 fusion.32
  250.9 45.1 %all-gather.21.cloned.1.call-done = f32[4096,128]{0,1:T(8,128)} async-done(((f32[1024,128]{0,1:T(8,128)}), f32[4096,128]{0,1:T(8,128)}) %all-gather.21.cloned.1.call-update) | async-done | bytes 2097168 | tf_op jit(solution)/shard_map/all_gather | solution.py:33
  303.6 51.9 %all-reduce.13.cloned.1.call-done = f32[256,128]{0,1:T(8,128)} async-done(((f32[256,128]{0,1:T(8,128)}), f32[256,128]{0,1:T(8,128)}) %all-reduce.13.cloned.1.call-update) | async-done | bytes 131088 | tf_op jit(solution)/shard_map/psum | solution.py:9
  355.5 7.8 fusion.33
  372.3 44.2 %all-gather.23.cloned.1.call-done = f32[4096,128]{0,1:T(8,128)} async-done(((f32[1024,128]{0,1:T(8,128)}), f32[4096,128]{0,1:T(8,128)}) %all-gather.23.cloned.1.call-update) | async-done | bytes 2097168 | tf_op jit(solution)/shard_map/all_gather | solution.py:33
  423.7 52.2 %all-reduce.15.cloned.1.call-done = f32[256,128]{0,1:T(8,128)} async-done(((f32[256,128]{0,1:T(8,128)}), f32[256,128]{0,1:T(8,128)}) %all-reduce.15.cloned.1.call-update) | async-done | bytes 131088 | tf_op jit(solution)/shard_map/psum | solution.py:9
  475.9 7.8 fusion.34
  483.8 5.0 fusion.10
  493.0 12.5 %fusion.100 = (bf16[1,256,8,1024]{3,2,1,0:T(8,128)(2,1)}, bf16[1,256,8,1024]{3,2,1,0:T(8,128)(2,1)}, bf16[1,256,8,1024]{3,2,1,0:T(8,128)(2,1)}, bf16[1,256,8,1024]{3,2,1,0:T(8,128)(2,1)}) fusion(bf16[4,256,8,1024]{3,2,1,0:T(8,128)(2,1)} %param.14), kind=kLoop, calls=%fused_computation.169 | loop fusion | bytes 33554432 | tf_op jit(solution)/shard_map/slice | solution.py:98
  505.4 31.5 %all-gather.25.cloned.1.call-done = f32[4096,128]{0,1:T(8,128)} async-done(((f32[1024,128]{0,1:T(8,128)}), f32[4096,128]{0,1:T(8,128)}) %all-gather.25.cloned.1.call-update) | async-done | bytes 2097168 | tf_op jit(solution)/shard_map/all_gather | solution.py:33
  543.7 52.1 %all-reduce.17.cloned.1.call-done = f32[256,128]{0,1:T(8,128)} async-done(((f32[256,128]{0,1:T(8,128)}), f32[256,128]{0,1:T(8,128)}) %all-reduce.17.cloned.1.call-update) | async-done | bytes 131088 | tf_op jit(solution)/shard_map/psum | solution.py:9
  595.9 7.3 fusion.23
  603.3 7.2 fusion.13
  613.9 44.7 %all-gather.27.cloned.1.call-done = f32[4096,128]{0,1:T(8,128)} async-done(((f32[1024,128]{0,1:T(8,128)}), f32[4096,128]{0,1:T(8,128)}) %all-gather.27.cloned.1.call-update) | async-done | bytes 2097168 | tf_op jit(solution)/shard_map/all_gather | solution.py:33
  665.2 52.4 %all-reduce.19.cloned.1.call-done = f32[256,128]{0,1:T(8,128)} async-done(((f32[256,128]{0,1:T(8,128)}), f32[256,128]{0,1:T(8,128)}) %all-reduce.19.cloned.1.call-update) | async-done | bytes 131088 | tf_op jit(solution)/shard_map/psum | solution.py:9
  717.6 7.3 fusion.25
  724.9 7.1 fusion.16
  735.3 45.0 %all-gather.29.cloned.1.call-done = f32[4096,128]{0,1:T(8,128)} async-done(((f32[1024,128]{0,1:T(8,128)}), f32[4096,128]{0,1:T(8,128)}) %all-gather.29.cloned.1.call-update) | async-done | bytes 2097168 | tf_op jit(solution)/shard_map/all_gather | solution.py:33
  786.9 52.4 %all-reduce.21.cloned.1.call-done = f32[256,128]{0,1:T(8,128)} async-done(((f32[256,128]{0,1:T(8,128)}), f32[256,128]{0,1:T(8,128)}) %all-reduce.21.cloned.1.call-update) | async-done | bytes 131088 | tf_op jit(solution)/shard_map/psum | solution.py:9
  839.2 7.3 fusion.27
  846.6 7.2 fusion.19
  856.9 44.9 %all-gather.31.cloned.1.call-done = f32[4096,128]{0,1:T(8,128)} async-done(((f32[1024,128]{0,1:T(8,128)}), f32[4096,128]{0,1:T(8,128)}) %all-gather.31.cloned.1.call-update) | async-done | bytes 2097168 | tf_op jit(solution)/shard_map/all_gather | solution.py:33
  908.5 52.4 %all-reduce.23.cloned.1.call-done = f32[256,128]{0,1:T(8,128)} async-done(((f32[256,128]{0,1:T(8,128)}), f32[256,128]{0,1:T(8,128)}) %all-reduce.23.cloned.1.call-update) | async-done | bytes 131088 | tf_op jit(solution)/shard_map/psum | solution.py:9
  960.8 7.3 fusion.29
  968.2 8.8 fusion.22
  979.9 73.4 %reduce-scatter.2.cloned.1.call-done = f32[8,256,128]{1,2,0:T(8,128)} async-done(((f32[8,1024,128]{1,2,0:T(8,128)}), f32[8,256,128]{1,2,0:T(8,128)}) %reduce-scatter.2.cloned.1.call-update) | async-done | bytes 1048592 | tf_op jit(solution)/shard_map/reduce_scatter | solution.py:106
  (184 shorter events, 99.8 us)
Async XLA Ops:
  7.2 51.4 %all-gather.17.cloned.1.call-start = ((), (), s32[]{:S(2)}) async-start(), calls=%async_computation.10 | async-start | bytes 2621440 | tf_op jit(solution)/shard_map/all_gather | solution.py:33
  8.8 43.1 %copy-start.19 = (f32[8,256,128]{1,2,0:T(8,128)}, f32[8,256,128]{1,2,0:T(8,128)S(1)}, u32[]{:S(2)}) copy-start(f32[8,256,128]{1,2,0:T(8,128)S(1)} %copy.26) | copy-start | bytes 3145732
  9.9 108.1 %all-reduce.9.cloned.1.call-start = ((), (), s32[]{:S(2)}) async-start(), calls=%async_computation.1 | async-start | bytes 262144 | tf_op jit(solution)/shard_map/psum | solution.py:9
  65.6 110.0 %all-gather.19.cloned.1.call-start = ((), (), s32[]{:S(2)}) async-start(), calls=%async_computation.11 | async-start | bytes 2621440 | tf_op jit(solution)/shard_map/all_gather | solution.py:33
  118.0 7.9 copy-start.4
  118.0 7.9 copy-start.21
  130.5 104.7 %all-reduce.11.cloned.1.call-start = ((), (), s32[]{:S(2)}) async-start(), calls=%async_computation.2 | async-start | bytes 262144 | tf_op jit(solution)/shard_map/psum | solution.py:9
  182.7 113.3 %all-gather.21.cloned.1.call-start = ((), (), s32[]{:S(2)}) async-start(), calls=%async_computation.12 | async-start | bytes 2621440 | tf_op jit(solution)/shard_map/all_gather | solution.py:33
  235.2 7.8 copy-start.18
  235.2 7.8 copy-start.22
  250.8 104.7 %all-reduce.13.cloned.1.call-start = ((), (), s32[]{:S(2)}) async-start(), calls=%async_computation.3 | async-start | bytes 262144 | tf_op jit(solution)/shard_map/psum | solution.py:9
  303.1 113.3 %all-gather.23.cloned.1.call-start = ((), (), s32[]{:S(2)}) async-start(), calls=%async_computation.13 | async-start | bytes 2621440 | tf_op jit(solution)/shard_map/all_gather | solution.py:33
  355.5 7.8 copy-start.12
  355.5 7.8 copy-start.23
  355.5 7.8 copy-start.39
  371.2 104.7 %all-reduce.15.cloned.1.call-start = ((), (), s32[]{:S(2)}) async-start(), calls=%async_computation.4 | async-start | bytes 262144 | tf_op jit(solution)/shard_map/psum | solution.py:9
  423.5 113.4 %all-gather.25.cloned.1.call-start = ((), (), s32[]{:S(2)}) async-start(), calls=%async_computation.14 | async-start | bytes 2621440 | tf_op jit(solution)/shard_map/all_gather | solution.py:33
  475.9 7.8 copy-start.8
  475.9 7.8 copy-start.24
  475.9 7.8 copy-start.37
  483.8 8.0 copy-start.45
  483.8 8.6 copy-start.43
  491.7 104.2 %all-reduce.17.cloned.1.call-start = ((), (), s32[]{:S(2)}) async-start(), calls=%async_computation.5 | async-start | bytes 262144 | tf_op jit(solution)/shard_map/psum | solution.py:9
  543.4 115.1 %all-gather.27.cloned.1.call-start = ((), (), s32[]{:S(2)}) async-start(), calls=%async_computation.15 | async-start | bytes 2621440 | tf_op jit(solution)/shard_map/all_gather | solution.py:33
  613.4 104.2 %all-reduce.19.cloned.1.call-start = ((), (), s32[]{:S(2)}) async-start(), calls=%async_computation.6 | async-start | bytes 262144 | tf_op jit(solution)/shard_map/psum | solution.py:9
  665.1 115.1 %all-gather.29.cloned.1.call-start = ((), (), s32[]{:S(2)}) async-start(), calls=%async_computation.16 | async-start | bytes 2621440 | tf_op jit(solution)/shard_map/all_gather | solution.py:33
  717.5 7.4 copy-start.40
  735.0 104.2 %all-reduce.21.cloned.1.call-start = ((), (), s32[]{:S(2)}) async-start(), calls=%async_computation.7 | async-start | bytes 262144 | tf_op jit(solution)/shard_map/psum | solution.py:9
  786.8 115.1 %all-gather.31.cloned.1.call-start = ((), (), s32[]{:S(2)}) async-start(), calls=%async_computation.17 | async-start | bytes 2621440 | tf_op jit(solution)/shard_map/all_gather | solution.py:33
  856.7 104.2 %all-reduce.23.cloned.1.call-start = ((), (), s32[]{:S(2)}) async-start(), calls=%async_computation.8 | async-start | bytes 262144 | tf_op jit(solution)/shard_map/psum | solution.py:9
  908.4 144.9 %reduce-scatter.2.cloned.1.call-start = ((), (), s32[]{:S(2)}) async-start(), calls=%async_computation.9 | async-start | bytes 5242880 | tf_op jit(solution)/shard_map/reduce_scatter | solution.py:106
  977.0 76.4 %copy-start.20 = (f32[8,256,128]{1,2,0:T(8,128)S(1)}, f32[8,256,128]{1,2,0:T(8,128)}, u32[]{:S(2)}) copy-start(f32[8,256,128]{1,2,0:T(8,128)} %copy-done.19) | copy-start | bytes 3145732
  (31 other events, 164.5 us)
Sparse Core Ops, SparseCore 0:
  10.1 48.3 all-gather.16
  65.8 52.2 all-reduce.8
  130.6 45.0 all-gather.18
  182.9 52.2 all-reduce.10
  250.9 45.0 all-gather.20
  303.2 52.2 all-reduce.12
  371.3 45.0 all-gather.22
  423.6 52.2 all-reduce.14
  491.8 45.0 all-gather.24
  543.6 52.2 all-reduce.16
  613.5 45.0 all-gather.26
  665.2 52.2 all-reduce.18
  735.2 45.0 all-gather.28
  786.9 52.2 all-reduce.20
  856.8 45.0 all-gather.30
  908.5 52.2 all-reduce.22
  977.1 76.1 reduce-scatter.1
